TPU v7x, 32 devices: a whole 2x2x4 slice. The times are simulated.
32 devices in a mesh: groups: 2 (over x), seq: 8 (over z, y), head: 2 (over core).
Axes of the slice: x: 2, y: 2, z: 4, core: 2. Of those that a mesh axis runs over, the one named last changes fastest.
Arguments:
- q_latent: bfloat16 [16, 64, 512], P(('groups', 'seq'), 'head'), parts along dimension 0, may hold values from -7.5 to 7.5
- q_rope: bfloat16 [16, 4096], P(('groups', 'seq'), 'head'), parts along dimension 0, may hold values from -7.5 to 7.5
- cache_latent: bfloat16 [768, 64, 512], P(('groups', 'seq', 'head')), parts along dimension 0, may hold values from -10 to 10
- cache_rope: bfloat16 [768, 4096], P(('groups', 'seq', 'head')), parts along dimension 0, may hold values from -6 to 6
- page_table: int32 [16, 48], P('groups'), parts along dimension 0, may hold values from 0 to 383, as said below
- lengths: int32 [16], P('groups'), parts along dimension 0, may hold values from 1 to 3072, 14745 in all
Outputs:
- attended: bfloat16 [16, 64, 512], P(('groups', 'seq'), 'head'), parts along dimension 0
There are 2 independent parts, one for each index of `groups`. A program takes and returns all parts, laid end to end along the dimension named above; each array names one. Nothing has to cross between parts.
Inputs may be any that keep to these rules, and one draw needn't show every extreme that they name: `page_table`: device d of a group (d = seq index * 2 + head index) holds pool pages d * 24 to (d + 1) * 24 - 1. Each pool page is named exactly once. A request's logical pages k * 3 to (k + 1) * 3 - 1 lie on one device, and every device holds exactly one such run of every request. `lengths`: the newest token is counted.
All inputs are finite; a program needn't handle non-finite values.
Results may differ from a plain program's by a relative error of at most 0.0055.
Values may be sent and summed in bfloat16 or wider, within the bound.
A program may use at most 128 MiB of HBM per device.

v0:
```python
import math

import jax
import jax.numpy as jnp
from jax import lax
from jax.sharding import PartitionSpec as P

ROPE = 64
NOPE = 128


MASKED_SCORE = -1e30


def softmax_update(carried, query_lat, query_rot, key_rows, rotary, live_mask, score_scale):
    row_max, row_total, summed = carried
    scores = jnp.einsum("hd,td->ht", query_lat, key_rows, preferred_element_type=jnp.float32)
    scores = (
        scores + jnp.einsum("hd,td->ht", query_rot, rotary, preferred_element_type=jnp.float32)
    ) * score_scale
    scores = jnp.where(live_mask[None, :], scores, MASKED_SCORE)
    new_max = jnp.maximum(row_max, jnp.max(scores, axis=1))
    exp_terms = jnp.where(live_mask[None, :], jnp.exp(scores - new_max[:, None]), 0.0)
    weights = exp_terms.astype(jnp.bfloat16)
    summed = jnp.dot(weights, key_rows, preferred_element_type=jnp.float32)
    return (new_max, jnp.sum(exp_terms, axis=1), summed)


def local(q_latent, q_rope, cache_latent, cache_rope, page_table, lengths):
    seq_count = lax.axis_size("seq")
    head_count = lax.axis_size("head")
    my_seq = lax.axis_index("seq")
    my_core = lax.axis_index("head")
    my_device = my_seq * head_count + my_core
    pool_pages, page_len, latent_width = cache_latent.shape
    rope_width = cache_rope.shape[1] // page_len
    request_count, page_slots = page_table.shape
    device_count = seq_count * head_count
    run_len = page_slots // device_count
    run_owner = page_table[:, ::run_len] // pool_pages
    device_ids = jnp.arange(device_count, dtype=jnp.int32)
    run_index = jnp.sum(jnp.where(run_owner == my_device, device_ids[None, :], 0), axis=1)
    offsets = jnp.arange(run_len, dtype=jnp.int32)
    slot_cols = run_index[:, None] * run_len + offsets[None, :]
    local_slots = jnp.take_along_axis(page_table, slot_cols, axis=1) - my_device * pool_pages
    flat_slots = local_slots.reshape(-1)
    picked_lat = cache_latent[flat_slots].reshape(request_count, run_len, page_len, latent_width)
    picked_rot = cache_rope[flat_slots].reshape(request_count, run_len, page_len * rope_width)
    score_scale = 1.0 / math.sqrt(NOPE + ROPE)
    token_ids = jnp.arange(page_len, dtype=jnp.int32)
    arrived = (
        lax.all_to_all(picked_lat, "seq", split_axis=0, concat_axis=1, tiled=True),
        lax.all_to_all(picked_rot, "seq", split_axis=0, concat_axis=1, tiled=True),
    )
    own_length = lengths[my_seq]
    own_owner = run_owner[my_seq]
    run_of_device = jnp.sum(
        jnp.where(own_owner[None, :] == device_ids[:, None], device_ids[None, :], 0), axis=1
    )
    heads_here = q_latent.shape[1]
    query_lat = q_latent[0]
    query_rot = q_rope[0].reshape(heads_here, rope_width)
    per_core = seq_count * run_len
    start_carry = (
        jnp.full((heads_here,), MASKED_SCORE, jnp.float32),
        jnp.zeros((heads_here,), jnp.float32),
        jnp.zeros((heads_here, latent_width), jnp.float32),
    )
    piece_lat = lax.all_gather(arrived[0], "head", axis=1, tiled=True)
    piece_rot = lax.all_gather(arrived[1], "head", axis=1, tiled=True)
    piece_count = piece_lat.shape[1]
    gathered = jnp.arange(piece_count, dtype=jnp.int32)
    source_core = gathered // per_core
    within = gathered % per_core
    source = within // run_len * head_count + source_core
    page_start = (run_of_device[source] * run_len + within % run_len) * page_len
    positions = (page_start[:, None] + token_ids[None, :]).reshape(-1)
    live_mask = positions < own_length
    key_rows = piece_lat.reshape(piece_count * page_len, latent_width)
    rotary = piece_rot.reshape(piece_count * page_len, rope_width)
    row_max, row_total, summed = softmax_update(
        start_carry, query_lat, query_rot, key_rows, rotary, live_mask, score_scale
    )
    return (summed / row_total[:, None]).astype(jnp.bfloat16)[None]


def solution(mesh):
    return jax.shard_map(
        local,
        mesh=mesh,
        in_specs=(
            P(("groups", "seq"), "head", None),
            P(("groups", "seq"), "head"),
            P(("groups", "seq", "head"), None, None),
            P(("groups", "seq", "head"), None),
            P("groups", None),
            P("groups"),
        ),
        out_specs=P(("groups", "seq"), "head", None),
        check_vma=False,
    )
```

profile of v0, /device:TPU:0, one launch (start us, length us, event | category | flops | bytes accessed | tf_op | source)
XLA Modules:
  0.0 83.4 jit_solution(11498527822076780127)
XLA Ops:
  6.5 0.9 %slice.3 = s32[8,16]{1,0:T(8,128)S(1)} slice(s32[8,48]{1,0:T(8,128)} %param.10), slice={[0:8:1], [0:48:3]} | slice | bytes 1024 | tf_op jit(solution)/shard_map/slice | solution.py:40
  7.4 0.1 select_reduce_fusion.1
  7.6 0.1 reshape.281
  7.7 1.5 %gather_fusion.3 = s32[24]{0:T(128)S(1)} fusion(s32[8,48]{1,0:T(8,128)} %param.10, s32[24]{0:T(128)S(1)} %reshape.281), kind=kCustom, calls=%fused_computation.3 | custom fusion | bytes 384 | tf_op jit(solution)/shard_map/jit(take_along_axis)/gather | solution.py:45
  9.3 0.1 add.190
  9.5 0.6 gather_fusion.1
  10.2 44.3 %all_to_all.24 = bf16[8,3,64,512]{3,2,1,0:T(8,128)(2,1)} all-to-all(bf16[8,3,64,512]{3,2,1,0:T(8,128)(2,1)S(1)} %bitcast.34), channel_id=1, replica_groups=mesh['groups'=2,'seq'=8,'head'=2] {'seq'}, dimensions={0} | all-to-all | bytes 3145728 | tf_op jit(solution)/shard_map/all_to_all | solution.py:52
  54.6 0.7 gather_fusion.2
  55.3 0.8 %reshape.255 = bf16[8,3,4096]{2,1,0:T(4,128)(2,1)} reshape(bf16[24,4096]{1,0:T(8,128)(2,1)S(1)} %gather_fusion.2) | data formatting | bytes 393216 | tf_op jit(solution)/shard_map/reshape | solution.py:48
  56.1 3.6 %all-to-all-start.1 = ((bf16[8,3,4096]{2,1,0:T(4,128)(2,1)}), bf16[8,3,4096]{2,1,0:T(4,128)(2,1)S(1)}, u32[]{:S(2)}, u32[]{:S(2)}) async-start(bf16[8,3,4096]{2,1,0:T(4,128)(2,1)} %reshape.255), calls=%async_computation.1 | async-start | bytes 524288 | tf_op jit(solution)/shard_map/all_to_all | solution.py:53
  59.7 0.6 dynamic_slice.7
  60.3 0.1 select_reduce_fusion
  60.5 0.8 gather_fusion
  61.3 0.7 add_compare_fusion
  62.0 0.1 lt.81
  62.1 0.1 reshape_squeeze.3
  62.2 6.1 %all-to-all-done.1 = bf16[8,3,4096]{2,1,0:T(4,128)(2,1)S(1)} async-done(((bf16[8,3,4096]{2,1,0:T(4,128)(2,1)}), bf16[8,3,4096]{2,1,0:T(4,128)(2,1)S(1)}, u32[]{:S(2)}, u32[]{:S(2)}) %all-to-all-start.1) | async-done | bytes 196640 | tf_op jit(solution)/shard_map/all_to_all | solution.py:53
  68.3 0.2 all_to_all.21
  68.4 2.1 %all_gather.7 = bf16[1,48,4096]{2,1,0:T(8,128)(2,1)S(1)} all-gather(bf16[1,24,4096]{2,1,0:T(8,128)(2,1)S(1)} %all_to_all.21), channel_id=1, replica_groups=mesh['groups'=2,'seq'=8,'head'=2] {'head'}, dimensions={1}, use_global_device_ids=true | all-gather | bytes 589824 | tf_op jit(solution)/shard_map/all_gather | solution.py:70
  70.5 0.8 %reshape.256 = bf16[3072,64]{1,0:T(8,128)(2,1)S(1)} reshape(bf16[1,48,4096]{2,1,0:T(8,128)(2,1)S(1)} %all_gather.7) | data formatting | bytes 786432 | tf_op jit(solution)/shard_map/reshape | solution.py:80
  71.4 0.4 fusion.23
  71.8 3.2 %fusion.22 = (f32[32]{0:T(128)S(1)}, f32[3072,32]{0,1:T(8,128)S(1)}) fusion(f32[3072,32]{0,1:T(8,128)S(1)} %fusion.23, bf16[3072,512]{1,0:T(8,128)(2,1)} %bitcast.31, bf16[1,32,512]{2,1,0:T(8,128)(2,1)S(1)} %copy-done.3, pred[3072]{0:T(1024)(128)(4,1)S(1)} %lt.81), kind=kOutput, calls=%fused_computation.53 | convolution fusion | flops 101056480 | bytes 3968128 | tf_op jit(solution)/shard_map/hd,td->ht/dot_general | solution.py:17
  75.0 0.3 fusion.4
  75.2 1.3 %fusion.3 = bf16[1,32,512]{2,1,0:T(8,128)(2,1)} fusion(bf16[3072,512]{1,0:T(8,128)(2,1)S(1)} %bitcast.32, f32[3072,32]{0,1:T(8,128)S(1)} %get-tuple-element.8, f32[32]{0:T(128)S(1)} %broadcast_maximum_fusion, pred[3072]{0:T(1024)(128)(4,1)S(1)} %lt.81, f32[32]{0:T(128)S(1)} %fusion.4), kind=kOutput, calls=%fused_computation.9 | convolution fusion | flops 100990976 | bytes 3575040 | tf_op jit(solution)/shard_map/dot_general | solution.py:25
  (28 shorter events, 0.4 us)
Async XLA Ops:
  6.5 3.0 %copy-start = (bf16[24,64,512]{2,1,0:T(8,128)(2,1)S(1)}, bf16[24,64,512]{2,1,0:T(8,128)(2,1)}, u32[]{:S(2)}) copy-start(bf16[24,64,512]{2,1,0:T(8,128)(2,1)} %param.8) | copy-start | bytes 4718596
  6.5 65.2 %all-gather.2.cloned.1.call-start = ((), (), s32[]{:S(2)}) async-start(), calls=%async_computation.2 | async-start | bytes 4718592 | tf_op jit(solution)/shard_map/all_gather | solution.py:69
  10.2 44.4 %copy-start.2 = (bf16[24,4096]{1,0:T(8,128)(2,1)S(1)}, bf16[24,4096]{1,0:T(8,128)(2,1)}, u32[]{:S(2)}) copy-start(bf16[24,4096]{1,0:T(8,128)(2,1)} %param.9) | copy-start | bytes 589828
  10.2 49.5 %copy-start.5 = (s32[8]{0:T(128)S(1)}, s32[8]{0:T(128)}, u32[]{:S(2)}) copy-start(s32[8]{0:T(128)} %param.11) | copy-start | bytes 100
  54.5 7.5 %copy-start.4 = (bf16[1,2048]{1,0:T(2,128)(2,1)S(1)}, bf16[1,2048]{1,0:T(2,128)(2,1)}, u32[]{:S(2)}) copy-start(bf16[1,2048]{1,0:T(2,128)(2,1)} %param.7) | copy-start | bytes 12292
  54.6 17.2 %copy-start.3 = (bf16[1,32,512]{2,1,0:T(8,128)(2,1)S(1)}, bf16[1,32,512]{2,1,0:T(8,128)(2,1)}, u32[]{:S(2)}) copy-start(bf16[1,32,512]{2,1,0:T(8,128)(2,1)} %param.6) | copy-start | bytes 98308
  56.1 12.2 %all-to-all-start.1 = ((bf16[8,3,4096]{2,1,0:T(4,128)(2,1)}), bf16[8,3,4096]{2,1,0:T(4,128)(2,1)S(1)}, u32[]{:S(2)}, u32[]{:S(2)}) async-start(bf16[8,3,4096]{2,1,0:T(4,128)(2,1)} %reshape.255), calls=%async_computation.1 | async-start | bytes 524288 | tf_op jit(solution)/shard_map/all_to_all | solution.py:53
  71.7 3.5 %copy-start.1 = (bf16[1,48,64,512]{3,2,0,1:T(8,128)(2,1)S(1)}, bf16[1,48,64,512]{3,2,0,1:T(8,128)(2,1)}, u32[]{:S(2)}) copy-start(bf16[1,48,64,512]{3,2,0,1:T(8,128)(2,1)} %all-gather.2.cloned.1.call-done) | copy-start | bytes 9437188
Sparse Core Ops, SparseCore 0:
  54.7 11.1 all-gather.1
where the time goes:
time: 83.7 us; the launch traced here: 83.4 us
  blocking collectives  46.4 us (55%)
  between operations  13.6 us (16%)
  local copies, waits for them, and re-layouts  7.45 us (9%)
  waiting for transfers between devices  6.07 us (7%)
  matrix products  4.85 us (6%)
  starting transfers between devices  3.6 us (4%)
  other arithmetic  1.42 us (2%)
    all_to_all x1, blocking collectives, local(): lax.all_to_all(picked_lat, 'seq', split_axis=0, concat_axis=1, tiled=True)  44.3 us
    all_to_all x1, waiting for transfers between devices, local(): lax.all_to_all(picked_rot, 'seq', split_axis=0, concat_axis=1, tiled=True)  6.05 us
    all_to_all x1, starting transfers between devices, local(): lax.all_to_all(picked_rot, 'seq', split_axis=0, concat_axis=1, tiled=True)  3.59 us
    dot_general x1, matrix products, softmax_update(): jnp.einsum('hd,td->ht', query_lat, key_rows, preferred_element_type=jnp.f...  3.18 us
    all_gather x1, blocking collectives, local(): piece_rot = lax.all_gather(arrived[1], 'head', axis=1, tiled=True)  2.09 us
  transfers between devices with their start and end apart: 2, of which 1 were waited for; matrix products, arithmetic and copies ran while one was open for 6% of the time, Pallas kernels for 0%

commit v1 on v0

v1 whole, which is shorter than its diff:
```python
import functools
import math

import jax
import jax.numpy as jnp
from jax import lax
from jax.experimental import pallas as pl
from jax.experimental.pallas import tpu as pltpu
from jax.sharding import PartitionSpec as P

ROPE = 64
NOPE = 128
LANES = 128
MASKED_SCORE = -1e30


def flip(index, mask, count):
    result = index
    bit = 1
    while bit < count:
        if mask & bit:
            result = result + bit * (1 - 2 * ((index // bit) % 2))
        bit *= 2
    return result


def kernel(
    seq_count,
    run_len,
    qlat_hbm,
    qrot_hbm,
    lat_hbm,
    rot_hbm,
    table_hbm,
    len_hbm,
    out_ref,
    cache,
    rot_raw,
    rot_wide,
    rot_keys,
    qlat,
    qrot,
    qrot_rows,
    qrot_wide,
    part_send,
    part_recv,
    stat_send,
    stat_recv,
    table,
    lens,
    picks,
    local_sem,
    page_send_sem,
    page_recv_sem,
    q_send_sem,
    q_recv_sem,
    p_send_sem,
    p_recv_sem,
):
    me = lax.axis_index("seq")
    core = lax.axis_index("head")
    pool, page_len, latent = lat_hbm.shape
    heads = qlat.shape[1]
    rope = qrot.shape[2] // heads
    per_row = LANES // rope
    requests, slots = table.shape
    runs = slots // run_len
    scale = 1.0 / math.sqrt(NOPE + ROPE)

    loads = [
        pltpu.make_async_copy(qlat_hbm, qlat.at[pl.ds(0, 1)], local_sem.at[0]),
        pltpu.make_async_copy(qrot_hbm, qrot.at[0], local_sem.at[1]),
        pltpu.make_async_copy(table_hbm, table, local_sem.at[2]),
        pltpu.make_async_copy(len_hbm, lens, local_sem.at[3]),
        pltpu.make_async_copy(rot_hbm, rot_raw.at[0], local_sem.at[4]),
        pltpu.make_async_copy(lat_hbm, cache.at[0], local_sem.at[5]),
    ]
    for load in loads:
        load.start()

    barrier = pltpu.get_barrier_semaphore()
    for k in range(1, seq_count):
        pl.semaphore_signal(barrier, inc=1, device_id={"seq": flip(me, k, seq_count)})
    pl.semaphore_signal(barrier, inc=1, device_id={"head": 1 - core})

    loads[2].wait()
    loads[3].wait()
    base0 = (me * 2 + core) * pool
    base1 = (me * 2 + 1 - core) * pool

    chunk = math.gcd(runs, 16)

    def find(r, carry):
        def scan(c, found):
            run0, run1 = found
            for i in range(chunk):
                run = c * chunk + i
                first = table[r, run * run_len]
                run0 = jnp.where((first >= base0) & (first < base0 + pool), run, run0)
                run1 = jnp.where((first >= base1) & (first < base1 + pool), run, run1)
            return run0, run1

        zero = jnp.int32(0)
        if runs == chunk:
            run0, run1 = scan(0, (zero, zero))
        else:
            run0, run1 = lax.fori_loop(0, runs // chunk, scan, (zero, zero))
        for j in range(run_len):
            slot0 = table[r, run0 * run_len + j] - base0
            slot1 = table[r, run1 * run_len + j] - base1
            picks[r, j] = jnp.clip(slot0, 0, pool - 1)
            picks[r, run_len + j] = jnp.clip(slot1, 0, pool - 1)
        picks[r, 2 * run_len] = run0 * (run_len * page_len)
        picks[r, 2 * run_len + 1] = run1 * (run_len * page_len)
        return carry

    lax.fori_loop(0, requests, find, 0)

    loads[0].wait()
    loads[1].wait()
    pl.semaphore_wait(barrier, seq_count)

    q_copies = {}
    for k in range(1, seq_count):
        peer = {"seq": flip(me, k, seq_count)}
        q_copies[k] = (
            pltpu.make_async_remote_copy(
                qlat.at[0], qlat.at[k], q_send_sem.at[0, k], q_recv_sem.at[0, k], device_id=peer
            ),
            pltpu.make_async_remote_copy(
                qrot.at[0], qrot.at[k], q_send_sem.at[1, k], q_recv_sem.at[1, k], device_id=peer
            ),
        )
        for copy in q_copies[k]:
            copy.start()
    other = {"head": 1 - core}
    page_copies = (
        pltpu.make_async_remote_copy(
            rot_hbm, rot_raw.at[1], page_send_sem.at[0], page_recv_sem.at[0], device_id=other
        ),
        pltpu.make_async_remote_copy(
            lat_hbm, cache.at[1], page_send_sem.at[1], page_recv_sem.at[1], device_id=other
        ),
    )
    for copy in page_copies:
        copy.start()

    lane_block = lax.broadcasted_iota(jnp.int32, (pool, LANES), 1) // rope

    def spread(half):
        for j in range(page_len // per_row):
            tile = rot_raw[half, :, j * LANES : (j + 1) * LANES].astype(jnp.float32)
            for b in range(per_row):
                rot_wide[pl.ds(j * per_row + b, pool, stride=page_len), :] = jnp.where(
                    lane_block == b, tile, 0.0
                )

        def narrow(p, carry):
            start = pl.multiple_of(p * page_len, page_len)
            rot_keys[half, p] = rot_wide[pl.ds(start, page_len), :].astype(jnp.bfloat16)
            return carry

        lax.fori_loop(0, pool, narrow, 0)

    loads[4].wait()
    spread(0)
    page_copies[0].wait_recv()
    spread(1)
    loads[5].wait()
    page_copies[1].wait_recv()

    row_block = lax.broadcasted_iota(jnp.int32, (heads // per_row, LANES), 1) // rope
    tokens = 2 * run_len * page_len
    token = lax.broadcasted_iota(jnp.int32, (1, tokens), 1)
    stat_lane = lax.broadcasted_iota(jnp.int32, (heads, LANES), 1)

    def partial(k):
        r = flip(me, k, seq_count)
        for i in range(heads // per_row):
            qrot_rows[i : i + 1, :] = qrot[k, :, i * LANES : (i + 1) * LANES].astype(jnp.float32)
        rows = qrot_rows[...]
        for b in range(per_row):
            only = jnp.where(row_block == b, rows, 0.0)
            full = only
            for turn in range(1, per_row):
                full = full + pltpu.roll(only, turn * rope, 1)
            qrot_wide[pl.ds(b, heads // per_row, stride=per_row), :] = full
        query_rot = qrot_wide[...].astype(jnp.bfloat16)
        where = [(h, picks[r, h * run_len + j]) for h in range(2) for j in range(run_len)]
        keys = jnp.concatenate([cache[h, p] for h, p in where], axis=0)
        rots = jnp.concatenate([rot_keys[h, p] for h, p in where], axis=0)
        contract = (((1,), (1,)), ((), ()))
        scores = lax.dot_general(qlat[k], keys, contract, preferred_element_type=jnp.float32)
        scores = scores + lax.dot_general(
            query_rot, rots, contract, preferred_element_type=jnp.float32
        )
        scores = scores * scale
        start = jnp.where(
            token < tokens // 2, picks[r, 2 * run_len], picks[r, 2 * run_len + 1] - tokens // 2
        )
        live = start + token < lens[r]
        scores = jnp.where(live, scores, MASKED_SCORE)
        top = jnp.max(scores, axis=1, keepdims=True)
        terms = jnp.where(live, jnp.exp(scores - top), 0.0)
        total = jnp.sum(terms, axis=1, keepdims=True)
        summed = jnp.dot(terms.astype(jnp.bfloat16), keys, preferred_element_type=jnp.float32)
        stats = jnp.where(stat_lane == 0, top, jnp.where(stat_lane == 1, total, 0.0))
        return summed, jnp.transpose(stats)[:8, :]

    p_copies = {}
    for k in range(1, seq_count):
        q_copies[k][0].wait_recv()
        q_copies[k][1].wait_recv()
        summed, stats = partial(k)
        part_send[k] = summed.astype(jnp.bfloat16)
        stat_send[k, :, :heads] = stats
        peer = {"seq": flip(me, k, seq_count)}
        p_copies[k] = (
            pltpu.make_async_remote_copy(
                stat_send.at[k],
                stat_recv.at[k],
                p_send_sem.at[0, k],
                p_recv_sem.at[0, k],
                device_id=peer,
            ),
            pltpu.make_async_remote_copy(
                part_send.at[k],
                part_recv.at[k],
                p_send_sem.at[1, k],
                p_recv_sem.at[1, k],
                device_id=peer,
            ),
        )
        for copy in p_copies[k]:
            copy.start()
    own, stats = partial(0)
    stat_recv[0, :, :heads] = stats

    for k in range(1, seq_count):
        p_copies[k][0].wait_recv()
    tops = [stat_recv[k, 0:1, :heads] for k in range(seq_count)]
    top = functools.reduce(jnp.maximum, tops)
    weights = [jnp.exp(t - top) for t in tops]
    total = sum(w * stat_recv[k, 1:2, :heads] for k, w in enumerate(weights))
    weights = [w / total for w in weights]
    pad = -seq_count % 8
    stacked = jnp.concatenate(weights + [jnp.zeros((pad, heads), jnp.float32)] * (pad > 0), axis=0)
    columns = jnp.transpose(stacked)
    result = own * columns[:, 0:1]
    for k in range(1, seq_count):
        p_copies[k][1].wait_recv()
        result = result + part_recv[k].astype(jnp.float32) * columns[:, k : k + 1]
    out_ref[0] = result.astype(jnp.bfloat16)

    for k in range(1, seq_count):
        for copy in q_copies[k] + p_copies[k]:
            copy.wait_send()
    for copy in page_copies:
        copy.wait_send()


def local(q_latent, q_rope, cache_latent, cache_rope, page_table, lengths):
    seq_count = lax.axis_size("seq")
    head_count = lax.axis_size("head")
    pool, page_len, latent = cache_latent.shape
    heads = q_latent.shape[1]
    requests, slots = page_table.shape
    run_len = slots // (seq_count * head_count)
    anywhere = pl.BlockSpec(memory_space=pl.ANY)
    bf16, f32, i32 = jnp.bfloat16, jnp.float32, jnp.int32
    dma = pltpu.SemaphoreType.DMA
    return pl.pallas_call(
        functools.partial(kernel, seq_count, run_len),
        out_shape=jax.ShapeDtypeStruct(q_latent.shape, bf16),
        in_specs=[anywhere] * 6,
        out_specs=pl.BlockSpec(memory_space=pltpu.VMEM),
        scratch_shapes=[
            pltpu.VMEM((2, pool, page_len, latent), bf16),
            pltpu.VMEM((2,) + cache_rope.shape, bf16),
            pltpu.VMEM((pool * page_len, LANES), f32),
            pltpu.VMEM((2, pool, page_len, LANES), bf16),
            pltpu.VMEM((seq_count, heads, latent), bf16),
            pltpu.VMEM((seq_count, 1, q_rope.shape[1]), bf16),
            pltpu.VMEM((heads * cache_rope.shape[1] // page_len // LANES, LANES), f32),
            pltpu.VMEM((heads, LANES), f32),
            pltpu.VMEM((seq_count, heads, latent), bf16),
            pltpu.VMEM((seq_count, heads, latent), bf16),
            pltpu.VMEM((seq_count, 8, LANES), f32),
            pltpu.VMEM((seq_count, 8, LANES), f32),
            pltpu.SMEM((requests, slots), i32),
            pltpu.SMEM((requests,), i32),
            pltpu.SMEM((requests, 2 * run_len + 2), i32),
            dma((6,)),
            dma((2,)),
            dma((2,)),
            dma((2, seq_count)),
            dma((2, seq_count)),
            dma((2, seq_count)),
            dma((2, seq_count)),
        ],
        compiler_params=pltpu.CompilerParams(
            collective_id=0, has_side_effects=True, vmem_limit_bytes=60 * 2**20
        ),
    )(q_latent, q_rope, cache_latent, cache_rope, page_table, lengths)


def solution(mesh):
    return jax.shard_map(
        local,
        mesh=mesh,
        in_specs=(
            P(("groups", "seq"), "head", None),
            P(("groups", "seq"), "head"),
            P(("groups", "seq", "head"), None, None),
            P(("groups", "seq", "head"), None),
            P("groups", None),
            P("groups"),
        ),
        out_specs=P(("groups", "seq"), "head", None),
        check_vma=False,
    )
```

time: 83.7 us -> 22.9 us (0.27)
  blocking collectives: 46.4 us -> 0 us
  Pallas kernels: 0 us -> 21.4 us
  between operations: 13.6 us -> 0.01 us
  local copies, waits for them, and re-layouts: 7.45 us -> 1.38 us
  waiting for transfers between devices: 6.07 us -> 0 us
  matrix products: 4.85 us -> 0 us
  starting transfers between devices: 3.6 us -> 0 us
  other arithmetic: 1.42 us -> 0 us
    all_to_all x1 -> x0, blocking collectives: 44.3 us -> none  [local(): lax.all_to_all(picked_lat, 'seq', split_axis=0, concat_axis=1, tiled=True)]
    pallas_call x0 -> x1, Pallas kernels: none -> 21.4 us  [local(): pl.pallas_call(functools.partial(kernel, seq_count, run_len), out_shape=j...]
    all_to_all x1 -> x0, waiting for transfers between devices: 6.05 us -> none  [local(): lax.all_to_all(picked_rot, 'seq', split_axis=0, concat_axis=1, tiled=True)]
    dot_general x3 -> x0, matrix products: 4.85 us -> none  [the longest x1 3.18 us: softmax_update(): jnp.einsum('hd,td->ht', query_lat, key_rows, preferred_element_type=jnp.f...]
    gather x5 -> x0, local copies, waits for them, and re-layouts: 3.68 us -> none  [the longest x2 1.58 us: local(): jnp.take_along_axis(page_table, slot_cols, axis=1) - my_device * pool_pages]
    all_to_all x1 -> x0, starting transfers between devices: 3.59 us -> none  [local(): lax.all_to_all(picked_rot, 'seq', split_axis=0, concat_axis=1, tiled=True)]
    all_gather x1 -> x0, blocking collectives: 2.09 us -> none  [local(): piece_rot = lax.all_gather(arrived[1], 'head', axis=1, tiled=True)]
    reshape x2 -> x0, local copies, waits for them, and re-layouts: 1.68 us -> none  [the longest x1 0.84 us: local(): cache_rope[flat_slots]]
  transfers between devices with their start and end apart: 2 -> 0, of which waited for: 1 -> 0; matrix products, arithmetic and copies ran while one was open for 6% -> 0% of each run, Pallas kernels for 0% -> 0%
where the time goes in v1:
time: 22.9 us; the launch traced here: 22.7 us
  Pallas kernels  21.4 us (93%)
  local copies, waits for them, and re-layouts  1.38 us (6%)
    pallas_call x1, Pallas kernels, local(): pl.pallas_call(functools.partial(kernel, seq_count, run_len), out_shape=j...  21.4 us
    unnamed x1, local copies, waits for them, and re-layouts  1.38 us

profile of v1, /device:TPU:0, one launch (start us, length us, event | category | flops | bytes accessed | tf_op | source)
XLA Modules:
  0.0 22.7 jit_solution(11866169329210683915)
XLA Ops:
  0.0 21.4 %shard_map.64 = bf16[1,32,512]{2,1,0:T(8,128)(2,1)} custom-call(bf16[1,32,512]{2,1,0:T(8,128)(2,1)} %qlat_hbm.1, bf16[1,2048]{1,0:T(2,128)(2,1)} %qrot_hbm.1, bf16[24,64,512]{2,1,0:T(8,128)(2,1)} %lat_hbm.1, bf16[24,4096]{1,0:T(8,128)(2,1)} %rot_hbm.1, s32[8,48]{1,0:T(8,128)} %table_hbm.1, s32[8]{0:T(128)} %len_hbm.1), custom_call_target="tpu_custom_call" | custom-call | tf_op jit(solution)/shard_map/pallas_call | solution.py:272
  21.4 1.4 %copy.8 = bf16[1,32,512]{2,1,0:T(8,128)(2,1)} copy(bf16[1,32,512]{2,1,0:T(8,128)(2,1)} %shard_map.64) | data formatting | bytes 65536

commit v2 on v1

--- a/solution.py
+++ b/solution.py
@@ -12,16 +12,7 @@
 NOPE = 128
 LANES = 128
 MASKED_SCORE = -1e30
-
-
-def flip(index, mask, count):
-    result = index
-    bit = 1
-    while bit < count:
-        if mask & bit:
-            result = result + bit * (1 - 2 * ((index // bit) % 2))
-        bit *= 2
-    return result
+PAIR = 2
 
 
 def kernel(
@@ -78,10 +69,67 @@
     for load in loads:
         load.start()
 
+    ring = seq_count // PAIR
+    half_way = ring // 2
+    row, column = me // PAIR, me % PAIR
+
+    def slot(step, cross):
+        return (step % ring) * PAIR + cross
+
+    def index_of(step, cross):
+        col = 1 - column if cross else column
+        return ((row + step % ring) % ring) * PAIR + col
+
+    right, left, across = index_of(1, 0), index_of(-1, 0), index_of(0, 1)
     barrier = pltpu.get_barrier_semaphore()
-    for k in range(1, seq_count):
-        pl.semaphore_signal(barrier, inc=1, device_id={"seq": flip(me, k, seq_count)})
+    for peer in (right, left, across):
+        pl.semaphore_signal(barrier, inc=1, device_id={"seq": peer})
     pl.semaphore_signal(barrier, inc=1, device_id={"head": 1 - core})
+    loads[0].wait()
+    loads[1].wait()
+    pl.semaphore_wait(barrier, 4)
+
+    sent = []
+    arrivals = {}
+    first_rows, last_rows = pl.ds(0, heads // 2), pl.ds(heads // 2, heads // 2)
+
+    def push(ref, piece, source, target, peer, rows=None):
+        here, there = ref.at[source], ref.at[target]
+        if rows is not None:
+            here, there = ref.at[source, rows], ref.at[target, rows]
+        copy = pltpu.make_async_remote_copy(
+            here,
+            there,
+            q_send_sem.at[len(sent)],
+            q_recv_sem.at[piece, target],
+            device_id={"seq": peer},
+        )
+        copy.start()
+        sent.append(copy)
+        arrivals.setdefault(target, []).append(copy)
+
+    def push_all(source, target, peer):
+        push(qlat, 0, source, target, peer)
+        push(qrot, 1, source, target, peer)
+
+    def arrive(target, which=slice(None)):
+        for copy in arrivals[target][which]:
+            copy.wait_recv()
+
+    push_all(0, slot(-1, 0), right)
+    push_all(0, slot(1, 0), left)
+    push_all(0, slot(0, 1), across)
+    other = {"head": 1 - core}
+    page_copies = (
+        pltpu.make_async_remote_copy(
+            rot_hbm, rot_raw.at[1], page_send_sem.at[0], page_recv_sem.at[0], device_id=other
+        ),
+        pltpu.make_async_remote_copy(
+            lat_hbm, cache.at[1], page_send_sem.at[1], page_recv_sem.at[1], device_id=other
+        ),
+    )
+    for copy in page_copies:
+        copy.start()
 
     loads[2].wait()
     loads[3].wait()
@@ -116,35 +164,6 @@
 
     lax.fori_loop(0, requests, find, 0)
 
-    loads[0].wait()
-    loads[1].wait()
-    pl.semaphore_wait(barrier, seq_count)
-
-    q_copies = {}
-    for k in range(1, seq_count):
-        peer = {"seq": flip(me, k, seq_count)}
-        q_copies[k] = (
-            pltpu.make_async_remote_copy(
-                qlat.at[0], qlat.at[k], q_send_sem.at[0, k], q_recv_sem.at[0, k], device_id=peer
-            ),
-            pltpu.make_async_remote_copy(
-                qrot.at[0], qrot.at[k], q_send_sem.at[1, k], q_recv_sem.at[1, k], device_id=peer
-            ),
-        )
-        for copy in q_copies[k]:
-            copy.start()
-    other = {"head": 1 - core}
-    page_copies = (
-        pltpu.make_async_remote_copy(
-            rot_hbm, rot_raw.at[1], page_send_sem.at[0], page_recv_sem.at[0], device_id=other
-        ),
-        pltpu.make_async_remote_copy(
-            lat_hbm, cache.at[1], page_send_sem.at[1], page_recv_sem.at[1], device_id=other
-        ),
-    )
-    for copy in page_copies:
-        copy.start()
-
     lane_block = lax.broadcasted_iota(jnp.int32, (pool, LANES), 1) // rope
 
     def spread(half):
@@ -164,8 +183,34 @@
 
     loads[4].wait()
     spread(0)
+
+    def turn_back(step):
+        arrive(slot(step, 0))
+        push(qlat, 0, slot(step, 0), slot(half_way, 0), left, first_rows)
+        push(qrot, 1, slot(step, 0), slot(half_way, 0), left)
+        arrive(slot(-step, 0))
+        push(qlat, 2, slot(-step, 0), slot(half_way, 0), right, last_rows)
+
+    for step in range(1, half_way):
+        if step == half_way - 1:
+            turn_back(step)
+        else:
+            arrive(slot(step, 0))
+            push_all(slot(step, 0), slot(step + 1, 0), left)
+            arrive(slot(-step, 0))
+            push_all(slot(-step, 0), slot(-step - 1, 0), right)
+        arrive(slot(step - 1, 1))
+        push_all(slot(step - 1, 1), slot(step, 1), left)
+        if step > 1:
+            arrive(slot(1 - step, 1))
+        push_all(slot(1 - step, 1), slot(-step, 1), right)
     page_copies[0].wait_recv()
     spread(1)
+    arrive(slot(half_way, 0), slice(0, 2))
+    push(qlat, 0, slot(half_way, 0), slot(half_way, 1), across, first_rows)
+    push(qrot, 1, slot(half_way, 0), slot(half_way, 1), across)
+    arrive(slot(half_way, 0), slice(2, 3))
+    push(qlat, 2, slot(half_way, 0), slot(half_way, 1), across, last_rows)
     loads[5].wait()
     page_copies[1].wait_recv()
 
@@ -174,8 +219,7 @@
     token = lax.broadcasted_iota(jnp.int32, (1, tokens), 1)
     stat_lane = lax.broadcasted_iota(jnp.int32, (heads, LANES), 1)
 
-    def partial(k):
-        r = flip(me, k, seq_count)
+    def partial(k, r):
         for i in range(heads // per_row):
             qrot_rows[i : i + 1, :] = qrot[k, :, i * LANES : (i + 1) * LANES].astype(jnp.float32)
         rows = qrot_rows[...]
@@ -207,34 +251,44 @@
         stats = jnp.where(stat_lane == 0, top, jnp.where(stat_lane == 1, total, 0.0))
         return summed, jnp.transpose(stats)[:8, :]
 
+    order = [(0, 1)]
+    for step in range(1, half_way):
+        order += [(step, 0), (-step, 0)]
+    late = [(step * sign, 1) for step in range(1, half_way) for sign in (1, -1)]
+    order += [(0, 0)] + late + [(half_way, 0), (half_way, 1)]
+    relayed = {slot(step, 1) for step in range(half_way - 1)}
+    relayed |= {slot(-step, 1) for step in range(half_way - 1)}
     p_copies = {}
-    for k in range(1, seq_count):
-        q_copies[k][0].wait_recv()
-        q_copies[k][1].wait_recv()
-        summed, stats = partial(k)
+    for step, cross in order:
+        k, r = slot(step, cross), index_of(step, cross)
+        if k == 0:
+            own, stats = partial(0, me)
+            stat_recv[0, :, :heads] = stats
+            continue
+        if cross and k not in relayed:
+            arrive(k)
+        summed, stats = partial(k, r)
         part_send[k] = summed.astype(jnp.bfloat16)
         stat_send[k, :, :heads] = stats
-        peer = {"seq": flip(me, k, seq_count)}
+        back = slot(-step, cross)
         p_copies[k] = (
             pltpu.make_async_remote_copy(
                 stat_send.at[k],
-                stat_recv.at[k],
+                stat_recv.at[back],
                 p_send_sem.at[0, k],
-                p_recv_sem.at[0, k],
-                device_id=peer,
+                p_recv_sem.at[0, back],
+                device_id={"seq": r},
             ),
             pltpu.make_async_remote_copy(
                 part_send.at[k],
-                part_recv.at[k],
+                part_recv.at[back],
                 p_send_sem.at[1, k],
-                p_recv_sem.at[1, k],
-                device_id=peer,
+                p_recv_sem.at[1, back],
+                device_id={"seq": r},
             ),
         )
         for copy in p_copies[k]:
             copy.start()
-    own, stats = partial(0)
-    stat_recv[0, :, :heads] = stats
 
     for k in range(1, seq_count):
         p_copies[k][0].wait_recv()
@@ -247,15 +301,17 @@
     stacked = jnp.concatenate(weights + [jnp.zeros((pad, heads), jnp.float32)] * (pad > 0), axis=0)
     columns = jnp.transpose(stacked)
     result = own * columns[:, 0:1]
+    for step, cross in order:
+        k, back = slot(step, cross), slot(-step, cross)
+        if k > 0:
+            p_copies[k][1].wait_recv()
+            result = result + part_recv[back].astype(jnp.float32) * columns[:, back : back + 1]
+    out_ref[0] = result.astype(jnp.bfloat16)
+
     for k in range(1, seq_count):
-        p_copies[k][1].wait_recv()
-        result = result + part_recv[k].astype(jnp.float32) * columns[:, k : k + 1]
-    out_ref[0] = result.astype(jnp.bfloat16)
-
-    for k in range(1, seq_count):
-        for copy in q_copies[k] + p_copies[k]:
+        for copy in p_copies[k]:
             copy.wait_send()
-    for copy in page_copies:
+    for copy in sent + list(page_copies):
         copy.wait_send()
 
 
@@ -293,8 +349,8 @@
             dma((6,)),
             dma((2,)),
             dma((2,)),
-            dma((2, seq_count)),
-            dma((2, seq_count)),
+            dma((3 * seq_count,)),
+            dma((3, seq_count)),
             dma((2, seq_count)),
             dma((2, seq_count)),
         ],

time: 22.9 us -> 25.5 us (1.11)
  Pallas kernels: 21.4 us -> 23.9 us
    pallas_call x1, Pallas kernels: 21.4 us -> 23.9 us  [local(): pl.pallas_call(functools.partial(kernel, seq_count, run_len), out_shape=j...]
where the time goes in v2:
time: 25.5 us; the launch traced here: 25.3 us
  Pallas kernels  23.9 us (94%)
  local copies, waits for them, and re-layouts  1.38 us (5%)
    pallas_call x1, Pallas kernels, local(): pl.pallas_call(functools.partial(kernel, seq_count, run_len), out_shape=j...  23.9 us
    unnamed x1, local copies, waits for them, and re-layouts  1.38 us

profile of v2, /device:TPU:0, one launch (start us, length us, event | category | flops | bytes accessed | tf_op | source)
XLA Modules:
  0.0 25.3 jit_solution(12406799478280890794)
XLA Ops:
  0.0 23.9 %shard_map.64 = bf16[1,32,512]{2,1,0:T(8,128)(2,1)} custom-call(bf16[1,32,512]{2,1,0:T(8,128)(2,1)} %qlat_hbm.1, bf16[1,2048]{1,0:T(2,128)(2,1)} %qrot_hbm.1, bf16[24,64,512]{2,1,0:T(8,128)(2,1)} %lat_hbm.1, bf16[24,4096]{1,0:T(8,128)(2,1)} %rot_hbm.1, s32[8,48]{1,0:T(8,128)} %table_hbm.1, s32[8]{0:T(128)} %len_hbm.1), custom_call_target="tpu_custom_call" | custom-call | tf_op jit(solution)/shard_map/pallas_call | solution.py:328
  23.9 1.4 %copy.8 = bf16[1,32,512]{2,1,0:T(8,128)(2,1)} copy(bf16[1,32,512]{2,1,0:T(8,128)(2,1)} %shard_map.64) | data formatting | bytes 65536

commit v3 on v1

--- a/solution.py
+++ b/solution.py
@@ -120,19 +120,27 @@
     loads[1].wait()
     pl.semaphore_wait(barrier, seq_count)
 
-    q_copies = {}
-    for k in range(1, seq_count):
-        peer = {"seq": flip(me, k, seq_count)}
-        q_copies[k] = (
+    half_way, relayed = seq_count // 2, seq_count // 2 + 1
+    same = [k for k in range(2, seq_count, 2) if k != half_way]
+    cross = [k for k in range(3, seq_count, 2) if k != relayed]
+    sends = [half_way] + same + cross + [1]
+
+    def query_copies(source, target, peer):
+        copies = [
             pltpu.make_async_remote_copy(
-                qlat.at[0], qlat.at[k], q_send_sem.at[0, k], q_recv_sem.at[0, k], device_id=peer
-            ),
-            pltpu.make_async_remote_copy(
-                qrot.at[0], qrot.at[k], q_send_sem.at[1, k], q_recv_sem.at[1, k], device_id=peer
-            ),
-        )
-        for copy in q_copies[k]:
+                ref.at[source],
+                ref.at[target],
+                q_send_sem.at[part, target],
+                q_recv_sem.at[part, target],
+                device_id={"seq": flip(me, peer, seq_count)},
+            )
+            for part, ref in enumerate((qlat, qrot))
+        ]
+        for copy in copies:
             copy.start()
+        return tuple(copies)
+
+    q_copies = {k: query_copies(0, k, k) for k in sends}
     other = {"head": 1 - core}
     page_copies = (
         pltpu.make_async_remote_copy(
@@ -164,6 +172,9 @@
 
     loads[4].wait()
     spread(0)
+    for copy in q_copies[half_way]:
+        copy.wait_recv()
+    q_copies[relayed] = query_copies(half_way, relayed, 1)
     page_copies[0].wait_recv()
     spread(1)
     loads[5].wait()
@@ -205,12 +216,14 @@
         total = jnp.sum(terms, axis=1, keepdims=True)
         summed = jnp.dot(terms.astype(jnp.bfloat16), keys, preferred_element_type=jnp.float32)
         stats = jnp.where(stat_lane == 0, top, jnp.where(stat_lane == 1, total, 0.0))
-        return summed, jnp.transpose(stats)[:8, :]
+        return summed, jnp.transpose(stats)[:2, :]
 
     p_copies = {}
-    for k in range(1, seq_count):
-        q_copies[k][0].wait_recv()
-        q_copies[k][1].wait_recv()
+    order = sends + [relayed]
+    for k in order:
+        if k != half_way:
+            for copy in q_copies[k]:
+                copy.wait_recv()
         summed, stats = partial(k)
         part_send[k] = summed.astype(jnp.bfloat16)
         stat_send[k, :, :heads] = stats
@@ -247,7 +260,7 @@
     stacked = jnp.concatenate(weights + [jnp.zeros((pad, heads), jnp.float32)] * (pad > 0), axis=0)
     columns = jnp.transpose(stacked)
     result = own * columns[:, 0:1]
-    for k in range(1, seq_count):
+    for k in order:
         p_copies[k][1].wait_recv()
         result = result + part_recv[k].astype(jnp.float32) * columns[:, k : k + 1]
     out_ref[0] = result.astype(jnp.bfloat16)
@@ -285,8 +298,8 @@
             pltpu.VMEM((heads, LANES), f32),
             pltpu.VMEM((seq_count, heads, latent), bf16),
             pltpu.VMEM((seq_count, heads, latent), bf16),
-            pltpu.VMEM((seq_count, 8, LANES), f32),
-            pltpu.VMEM((seq_count, 8, LANES), f32),
+            pltpu.VMEM((seq_count, 2, LANES), f32),
+            pltpu.VMEM((seq_count, 2, LANES), f32),
             pltpu.SMEM((requests, slots), i32),
             pltpu.SMEM((requests,), i32),
             pltpu.SMEM((requests, 2 * run_len + 2), i32),

time: 22.9 us -> 21.9 us (0.956)
  Pallas kernels: 21.4 us -> 20.3 us
    pallas_call x1, Pallas kernels: 21.4 us -> 20.3 us  [local(): pl.pallas_call(functools.partial(kernel, seq_count, run_len), out_shape=j...]
where the time goes in v3:
time: 21.9 us; the launch traced here: 21.7 us
  Pallas kernels  20.3 us (93%)
  local copies, waits for them, and re-layouts  1.38 us (6%)
    pallas_call x1, Pallas kernels, local(): pl.pallas_call(functools.partial(kernel, seq_count, run_len), out_shape=j...  20.3 us
    unnamed x1, local copies, waits for them, and re-layouts  1.38 us

profile of v3, /device:TPU:0, one launch (start us, length us, event | category | flops | bytes accessed | tf_op | source)
XLA Modules:
  0.0 21.7 jit_solution(11881570037735293419)
XLA Ops:
  0.0 20.3 %shard_map.64 = bf16[1,32,512]{2,1,0:T(8,128)(2,1)} custom-call(bf16[1,32,512]{2,1,0:T(8,128)(2,1)} %qlat_hbm.1, bf16[1,2048]{1,0:T(2,128)(2,1)} %qrot_hbm.1, bf16[24,64,512]{2,1,0:T(8,128)(2,1)} %lat_hbm.1, bf16[24,4096]{1,0:T(8,128)(2,1)} %rot_hbm.1, s32[8,48]{1,0:T(8,128)} %table_hbm.1, s32[8]{0:T(128)} %len_hbm.1), custom_call_target="tpu_custom_call" | custom-call | tf_op jit(solution)/shard_map/pallas_call | solution.py:285
  20.4 1.4 %copy.8 = bf16[1,32,512]{2,1,0:T(8,128)(2,1)} copy(bf16[1,32,512]{2,1,0:T(8,128)(2,1)} %shard_map.64) | data formatting | bytes 65536
